TPU v7x, 64 devices: a 2x2x8 block of a 4x4x8 slice. The times are simulated.
64 devices in a mesh: dp: 4 (over x, y), cp: 16 (over z, core).
Axes of the slice: x: 2, y: 2, z: 8, core: 2. Of those that a mesh axis runs over, the one named last changes fastest.
The devices are a block of a 4x4x8 slice.
Arguments:
- q_tokens: bfloat16 [24576, 12, 128], P(('dp', 'cp')), parts along dimension 0
- k_tokens: bfloat16 [24576, 2, 128], P(('dp', 'cp')), parts along dimension 0
- v_tokens: bfloat16 [24576, 2, 128], P(('dp', 'cp')), parts along dimension 0
Outputs:
- output 1: bfloat16 [24576, 12, 128], P(('dp', 'cp')), parts along dimension 0
- output 2: float32 [24576, 12], P(('dp', 'cp')), parts along dimension 0
There are 4 independent parts. A program takes and returns all parts, laid end to end along the dimension named above; each array names one.
All inputs are finite; a program needn't handle non-finite values.
Results may differ from a plain program's by a relative error of at most 0.00257823.
Values are sent between devices in bfloat16 or wider.
A program may use at most 768 MiB of HBM per device.

v0:
```python
import jax
import jax.numpy as jnp
from jax import lax
from jax.sharding import PartitionSpec as P


def attend_update(q_blk, k_blk, v_blk, run_state, logit_scale, visible):
    acc, row_max, row_sum = run_state
    scores = jnp.einsum("qhgd,khd->hgqk", q_blk, k_blk, preferred_element_type=jnp.float32) * logit_scale
    if visible is not None:
        scores = jnp.where(visible, scores, -jnp.inf)
    new_max = jnp.maximum(row_max, jnp.max(scores, axis=-1))
    expd = jnp.exp(scores - new_max[..., None])
    rescale = jnp.exp(row_max - new_max)
    new_sum = row_sum * rescale + jnp.sum(expd, axis=-1)
    new_acc = acc * rescale[..., None] + jnp.einsum(
        "hgqk,khd->hgqd", expd.astype(jnp.bfloat16), v_blk, preferred_element_type=jnp.float32)
    return new_acc, new_max, new_sum


def solution(mesh):
    n_cp = mesh.shape["cp"]
    shift_pairs = [(source, (source + 1) % n_cp) for source in range(n_cp)]
    row_spec = P(("dp", "cp"), None, None)
    lse_spec = P(("dp", "cp"), None)

    def local_attention(q_tok, k_tok, v_tok):
        tok_count, q_heads, head_dim = q_tok.shape
        kv_heads = k_tok.shape[1]
        group_size = q_heads // kv_heads
        half_len = tok_count // 2
        logit_scale = head_dim ** -0.5
        my_index = lax.axis_index("cp")
        q_grp = q_tok.reshape(tok_count, kv_heads, group_size, head_dim)
        q_first = q_grp[:half_len]
        q_second = q_grp[half_len:]
        offsets = jnp.arange(half_len)
        local_pos = jnp.concatenate(
            [my_index * half_len + offsets, (2 * n_cp - 1 - my_index) * half_len + offsets])

        def empty_state():
            return (jnp.zeros((kv_heads, group_size, half_len, head_dim), jnp.float32),
                    jnp.full((kv_heads, group_size, half_len), -jnp.inf, jnp.float32),
                    jnp.zeros((kv_heads, group_size, half_len), jnp.float32))

        first_vis = local_pos[:half_len, None] >= local_pos[None, :half_len]
        second_vis = local_pos[half_len:, None] >= local_pos[None, :]
        state_first = attend_update(q_first, k_tok[:half_len], v_tok[:half_len], empty_state(), logit_scale, first_vis)
        state_second = attend_update(q_second, k_tok, v_tok, empty_state(), logit_scale, second_vis)

        def lower_source(k_blk, v_blk, first_in, second_in):
            return (attend_update(q_first, k_blk[:half_len], v_blk[:half_len], first_in, logit_scale, None),
                    attend_update(q_second, k_blk[:half_len], v_blk[:half_len], second_in, logit_scale, None))

        def upper_source(k_blk, v_blk, first_in, second_in):
            return first_in, attend_update(q_second, k_blk, v_blk, second_in, logit_scale, None)

        def hop(step_idx, loop_state):
            k_cur, v_cur, first_in, second_in = loop_state
            k_cur, v_cur = lax.ppermute((k_cur, v_cur), "cp", shift_pairs)
            source = (my_index - step_idx) % n_cp
            first_out, second_out = lax.cond(
                source < my_index, lower_source, upper_source, k_cur, v_cur, first_in, second_in)
            return k_cur, v_cur, first_out, second_out

        loop_out = lax.fori_loop(1, n_cp, hop, (k_tok, v_tok, state_first, state_second))

        def finish(state_half):
            acc, row_max, row_sum = state_half
            return (acc / row_sum[..., None]).astype(jnp.bfloat16), row_max + jnp.log(row_sum)

        out_first, lse_first = finish(loop_out[2])
        out_second, lse_second = finish(loop_out[3])
        out_all = jnp.concatenate([out_first, out_second], axis=2)
        lse_all = jnp.concatenate([lse_first, lse_second], axis=2)
        out_tok = jnp.transpose(out_all, (2, 0, 1, 3)).reshape(tok_count, q_heads, head_dim)
        lse_tok = jnp.transpose(lse_all, (2, 0, 1)).reshape(tok_count, q_heads)
        return out_tok, lse_tok

    return jax.shard_map(local_attention, mesh=mesh, in_specs=(row_spec, row_spec, row_spec),
                         out_specs=(row_spec, lse_spec), check_vma=False)
```

profile of v0, /device:TPU:148, one launch (start us, length us, event | category | flops | bytes accessed | tf_op | source)
XLA Modules:
  0.0 227.8 jit_solution(15149547147489792795)
XLA Ops:
  9.1 1.8 convolution_add_fusion.2
  10.9 214.2 %while.29 = (s32[]{:T(128)}, bf16[384,2,128]{2,0,1:T(8,128)(2,1)}, bf16[384,2,128]{2,0,1:T(8,128)(2,1)}, f32[2,6,192,128]{3,2,1,0:T(8,128)S(1)}, f32[2,6,192]{2,...) while((s32[]{:T(128)}, bf16[384,2,128]{2,0,1:T(8,128)(2,1)}, ...), condition=%wide.region_13.14_spmd, body=%wide.region_4.13_spmd.sunk | while | flops 461251584 | bytes 20845164 | solution.py:66
  12.3 5.0 %collective-permute-done = bf16[384,2,128]{2,0,1:T(8,128)(2,1)S(1)} collective-permute-done((bf16[384,2,128]{2,0,1:T(8,128)(2,1)}, bf16[384,2,128]{2,0,1:T(8,128)(2,1)S(1)}, u32[]{:S(2)}, u32[]{:S(2)}) %collective-permute-start) | collective-permute-done | bytes 196640 | tf_op jit(solution)/shard_map/while/body/eval_jaxpr/ppermute | solution.py:60
  17.3 2.1 collective-permute-done.1
  19.4 5.3 %conditional.2 = (f32[2,6,192,128]{3,2,1,0:T(8,128)S(1)}, f32[2,6,192]{2,1,0:T(8,128)S(1)}, f32[2,6,192]{2,1,0:T(8,128)S(1)}, f32[2,6,192,128]{3,2,1,0:T(8,128)S...) conditional(s32[]{:T(128)} %convert_element_type.52, (bf16[384,2,128]{2,0,1:T(8,128)(2,1)S(1)}, ...), branch_computations={%region_5.7_spmd, %region_8.12_spmd} | conditional | flops 461251584 | bytes 18466920 | solution.py:62
  19.4 1.6 bitcast_reduce_fusion.2
  26.2 6.2 %collective-permute-done = bf16[384,2,128]{2,0,1:T(8,128)(2,1)S(1)} collective-permute-done((bf16[384,2,128]{2,0,1:T(8,128)(2,1)}, bf16[384,2,128]{2,0,1:T(8,128)(2,1)S(1)}, u32[]{:S(2)}, u32[]{:S(2)}) %collective-permute-start) | collective-permute-done | bytes 196640 | tf_op jit(solution)/shard_map/while/body/eval_jaxpr/ppermute | solution.py:60
  32.4 2.1 collective-permute-done.1
  34.5 5.3 %conditional.2 = (f32[2,6,192,128]{3,2,1,0:T(8,128)S(1)}, f32[2,6,192]{2,1,0:T(8,128)S(1)}, f32[2,6,192]{2,1,0:T(8,128)S(1)}, f32[2,6,192,128]{3,2,1,0:T(8,128)S...) conditional(s32[]{:T(128)} %convert_element_type.52, (bf16[384,2,128]{2,0,1:T(8,128)(2,1)S(1)}, ...), branch_computations={%region_5.7_spmd, %region_8.12_spmd} | conditional | flops 461251584 | bytes 18466920 | solution.py:62
  41.2 6.3 %collective-permute-done = bf16[384,2,128]{2,0,1:T(8,128)(2,1)S(1)} collective-permute-done((bf16[384,2,128]{2,0,1:T(8,128)(2,1)}, bf16[384,2,128]{2,0,1:T(8,128)(2,1)S(1)}, u32[]{:S(2)}, u32[]{:S(2)}) %collective-permute-start) | collective-permute-done | bytes 196640 | tf_op jit(solution)/shard_map/while/body/eval_jaxpr/ppermute | solution.py:60
  47.5 2.1 collective-permute-done.1
  49.6 5.3 %conditional.2 = (f32[2,6,192,128]{3,2,1,0:T(8,128)S(1)}, f32[2,6,192]{2,1,0:T(8,128)S(1)}, f32[2,6,192]{2,1,0:T(8,128)S(1)}, f32[2,6,192,128]{3,2,1,0:T(8,128)S...) conditional(s32[]{:T(128)} %convert_element_type.52, (bf16[384,2,128]{2,0,1:T(8,128)(2,1)S(1)}, ...), branch_computations={%region_5.7_spmd, %region_8.12_spmd} | conditional | flops 461251584 | bytes 18466920 | solution.py:62
  56.3 6.3 %collective-permute-done = bf16[384,2,128]{2,0,1:T(8,128)(2,1)S(1)} collective-permute-done((bf16[384,2,128]{2,0,1:T(8,128)(2,1)}, bf16[384,2,128]{2,0,1:T(8,128)(2,1)S(1)}, u32[]{:S(2)}, u32[]{:S(2)}) %collective-permute-start) | collective-permute-done | bytes 196640 | tf_op jit(solution)/shard_map/while/body/eval_jaxpr/ppermute | solution.py:60
  62.6 2.1 collective-permute-done.1
  64.7 5.3 %conditional.2 = (f32[2,6,192,128]{3,2,1,0:T(8,128)S(1)}, f32[2,6,192]{2,1,0:T(8,128)S(1)}, f32[2,6,192]{2,1,0:T(8,128)S(1)}, f32[2,6,192,128]{3,2,1,0:T(8,128)S...) conditional(s32[]{:T(128)} %convert_element_type.52, (bf16[384,2,128]{2,0,1:T(8,128)(2,1)S(1)}, ...), branch_computations={%region_5.7_spmd, %region_8.12_spmd} | conditional | flops 461251584 | bytes 18466920 | solution.py:62
  71.4 6.3 %collective-permute-done = bf16[384,2,128]{2,0,1:T(8,128)(2,1)S(1)} collective-permute-done((bf16[384,2,128]{2,0,1:T(8,128)(2,1)}, bf16[384,2,128]{2,0,1:T(8,128)(2,1)S(1)}, u32[]{:S(2)}, u32[]{:S(2)}) %collective-permute-start) | collective-permute-done | bytes 196640 | tf_op jit(solution)/shard_map/while/body/eval_jaxpr/ppermute | solution.py:60
  77.7 2.1 collective-permute-done.1
  79.8 5.3 %conditional.2 = (f32[2,6,192,128]{3,2,1,0:T(8,128)S(1)}, f32[2,6,192]{2,1,0:T(8,128)S(1)}, f32[2,6,192]{2,1,0:T(8,128)S(1)}, f32[2,6,192,128]{3,2,1,0:T(8,128)S...) conditional(s32[]{:T(128)} %convert_element_type.52, (bf16[384,2,128]{2,0,1:T(8,128)(2,1)S(1)}, ...), branch_computations={%region_5.7_spmd, %region_8.12_spmd} | conditional | flops 461251584 | bytes 18466920 | solution.py:62
  86.5 6.3 %collective-permute-done = bf16[384,2,128]{2,0,1:T(8,128)(2,1)S(1)} collective-permute-done((bf16[384,2,128]{2,0,1:T(8,128)(2,1)}, bf16[384,2,128]{2,0,1:T(8,128)(2,1)S(1)}, u32[]{:S(2)}, u32[]{:S(2)}) %collective-permute-start) | collective-permute-done | bytes 196640 | tf_op jit(solution)/shard_map/while/body/eval_jaxpr/ppermute | solution.py:60
  92.8 2.1 collective-permute-done.1
  94.9 5.3 %conditional.2 = (f32[2,6,192,128]{3,2,1,0:T(8,128)S(1)}, f32[2,6,192]{2,1,0:T(8,128)S(1)}, f32[2,6,192]{2,1,0:T(8,128)S(1)}, f32[2,6,192,128]{3,2,1,0:T(8,128)S...) conditional(s32[]{:T(128)} %convert_element_type.52, (bf16[384,2,128]{2,0,1:T(8,128)(2,1)S(1)}, ...), branch_computations={%region_5.7_spmd, %region_8.12_spmd} | conditional | flops 461251584 | bytes 18466920 | solution.py:62
  101.5 6.3 %collective-permute-done = bf16[384,2,128]{2,0,1:T(8,128)(2,1)S(1)} collective-permute-done((bf16[384,2,128]{2,0,1:T(8,128)(2,1)}, bf16[384,2,128]{2,0,1:T(8,128)(2,1)S(1)}, u32[]{:S(2)}, u32[]{:S(2)}) %collective-permute-start) | collective-permute-done | bytes 196640 | tf_op jit(solution)/shard_map/while/body/eval_jaxpr/ppermute | solution.py:60
  107.8 2.1 collective-permute-done.1
  110.0 5.3 %conditional.2 = (f32[2,6,192,128]{3,2,1,0:T(8,128)S(1)}, f32[2,6,192]{2,1,0:T(8,128)S(1)}, f32[2,6,192]{2,1,0:T(8,128)S(1)}, f32[2,6,192,128]{3,2,1,0:T(8,128)S...) conditional(s32[]{:T(128)} %convert_element_type.52, (bf16[384,2,128]{2,0,1:T(8,128)(2,1)S(1)}, ...), branch_computations={%region_5.7_spmd, %region_8.12_spmd} | conditional | flops 461251584 | bytes 18466920 | solution.py:62
  116.6 6.3 %collective-permute-done = bf16[384,2,128]{2,0,1:T(8,128)(2,1)S(1)} collective-permute-done((bf16[384,2,128]{2,0,1:T(8,128)(2,1)}, bf16[384,2,128]{2,0,1:T(8,128)(2,1)S(1)}, u32[]{:S(2)}, u32[]{:S(2)}) %collective-permute-start) | collective-permute-done | bytes 196640 | tf_op jit(solution)/shard_map/while/body/eval_jaxpr/ppermute | solution.py:60
  122.9 2.1 collective-permute-done.1
  125.0 5.3 %conditional.2 = (f32[2,6,192,128]{3,2,1,0:T(8,128)S(1)}, f32[2,6,192]{2,1,0:T(8,128)S(1)}, f32[2,6,192]{2,1,0:T(8,128)S(1)}, f32[2,6,192,128]{3,2,1,0:T(8,128)S...) conditional(s32[]{:T(128)} %convert_element_type.52, (bf16[384,2,128]{2,0,1:T(8,128)(2,1)S(1)}, ...), branch_computations={%region_5.7_spmd, %region_8.12_spmd} | conditional | flops 461251584 | bytes 18466920 | solution.py:62
  131.7 6.3 %collective-permute-done = bf16[384,2,128]{2,0,1:T(8,128)(2,1)S(1)} collective-permute-done((bf16[384,2,128]{2,0,1:T(8,128)(2,1)}, bf16[384,2,128]{2,0,1:T(8,128)(2,1)S(1)}, u32[]{:S(2)}, u32[]{:S(2)}) %collective-permute-start) | collective-permute-done | bytes 196640 | tf_op jit(solution)/shard_map/while/body/eval_jaxpr/ppermute | solution.py:60
  138.0 2.1 collective-permute-done.1
  140.1 3.6 %conditional.2 = (f32[2,6,192,128]{3,2,1,0:T(8,128)S(1)}, f32[2,6,192]{2,1,0:T(8,128)S(1)}, f32[2,6,192]{2,1,0:T(8,128)S(1)}, f32[2,6,192,128]{3,2,1,0:T(8,128)S...) conditional(s32[]{:T(128)} %convert_element_type.52, (bf16[384,2,128]{2,0,1:T(8,128)(2,1)S(1)}, ...), branch_computations={%region_5.7_spmd, %region_8.12_spmd} | conditional | flops 461251584 | bytes 18466920 | solution.py:62
  145.1 6.3 %collective-permute-done = bf16[384,2,128]{2,0,1:T(8,128)(2,1)S(1)} collective-permute-done((bf16[384,2,128]{2,0,1:T(8,128)(2,1)}, bf16[384,2,128]{2,0,1:T(8,128)(2,1)S(1)}, u32[]{:S(2)}, u32[]{:S(2)}) %collective-permute-start) | collective-permute-done | bytes 196640 | tf_op jit(solution)/shard_map/while/body/eval_jaxpr/ppermute | solution.py:60
  151.4 2.1 collective-permute-done.1
  153.5 3.6 %conditional.2 = (f32[2,6,192,128]{3,2,1,0:T(8,128)S(1)}, f32[2,6,192]{2,1,0:T(8,128)S(1)}, f32[2,6,192]{2,1,0:T(8,128)S(1)}, f32[2,6,192,128]{3,2,1,0:T(8,128)S...) conditional(s32[]{:T(128)} %convert_element_type.52, (bf16[384,2,128]{2,0,1:T(8,128)(2,1)S(1)}, ...), branch_computations={%region_5.7_spmd, %region_8.12_spmd} | conditional | flops 461251584 | bytes 18466920 | solution.py:62
  158.4 6.3 %collective-permute-done = bf16[384,2,128]{2,0,1:T(8,128)(2,1)S(1)} collective-permute-done((bf16[384,2,128]{2,0,1:T(8,128)(2,1)}, bf16[384,2,128]{2,0,1:T(8,128)(2,1)S(1)}, u32[]{:S(2)}, u32[]{:S(2)}) %collective-permute-start) | collective-permute-done | bytes 196640 | tf_op jit(solution)/shard_map/while/body/eval_jaxpr/ppermute | solution.py:60
  164.7 2.1 collective-permute-done.1
  166.8 3.6 %conditional.2 = (f32[2,6,192,128]{3,2,1,0:T(8,128)S(1)}, f32[2,6,192]{2,1,0:T(8,128)S(1)}, f32[2,6,192]{2,1,0:T(8,128)S(1)}, f32[2,6,192,128]{3,2,1,0:T(8,128)S...) conditional(s32[]{:T(128)} %convert_element_type.52, (bf16[384,2,128]{2,0,1:T(8,128)(2,1)S(1)}, ...), branch_computations={%region_5.7_spmd, %region_8.12_spmd} | conditional | flops 461251584 | bytes 18466920 | solution.py:62
  171.8 6.3 %collective-permute-done = bf16[384,2,128]{2,0,1:T(8,128)(2,1)S(1)} collective-permute-done((bf16[384,2,128]{2,0,1:T(8,128)(2,1)}, bf16[384,2,128]{2,0,1:T(8,128)(2,1)S(1)}, u32[]{:S(2)}, u32[]{:S(2)}) %collective-permute-start) | collective-permute-done | bytes 196640 | tf_op jit(solution)/shard_map/while/body/eval_jaxpr/ppermute | solution.py:60
  178.1 2.1 collective-permute-done.1
  180.2 3.6 %conditional.2 = (f32[2,6,192,128]{3,2,1,0:T(8,128)S(1)}, f32[2,6,192]{2,1,0:T(8,128)S(1)}, f32[2,6,192]{2,1,0:T(8,128)S(1)}, f32[2,6,192,128]{3,2,1,0:T(8,128)S...) conditional(s32[]{:T(128)} %convert_element_type.52, (bf16[384,2,128]{2,0,1:T(8,128)(2,1)S(1)}, ...), branch_computations={%region_5.7_spmd, %region_8.12_spmd} | conditional | flops 461251584 | bytes 18466920 | solution.py:62
  185.1 6.3 %collective-permute-done = bf16[384,2,128]{2,0,1:T(8,128)(2,1)S(1)} collective-permute-done((bf16[384,2,128]{2,0,1:T(8,128)(2,1)}, bf16[384,2,128]{2,0,1:T(8,128)(2,1)S(1)}, u32[]{:S(2)}, u32[]{:S(2)}) %collective-permute-start) | collective-permute-done | bytes 196640 | tf_op jit(solution)/shard_map/while/body/eval_jaxpr/ppermute | solution.py:60
  191.4 2.1 collective-permute-done.1
  193.5 3.6 %conditional.2 = (f32[2,6,192,128]{3,2,1,0:T(8,128)S(1)}, f32[2,6,192]{2,1,0:T(8,128)S(1)}, f32[2,6,192]{2,1,0:T(8,128)S(1)}, f32[2,6,192,128]{3,2,1,0:T(8,128)S...) conditional(s32[]{:T(128)} %convert_element_type.52, (bf16[384,2,128]{2,0,1:T(8,128)(2,1)S(1)}, ...), branch_computations={%region_5.7_spmd, %region_8.12_spmd} | conditional | flops 461251584 | bytes 18466920 | solution.py:62
  198.5 6.3 %collective-permute-done = bf16[384,2,128]{2,0,1:T(8,128)(2,1)S(1)} collective-permute-done((bf16[384,2,128]{2,0,1:T(8,128)(2,1)}, bf16[384,2,128]{2,0,1:T(8,128)(2,1)S(1)}, u32[]{:S(2)}, u32[]{:S(2)}) %collective-permute-start) | collective-permute-done | bytes 196640 | tf_op jit(solution)/shard_map/while/body/eval_jaxpr/ppermute | solution.py:60
  204.8 2.1 collective-permute-done.1
  206.9 3.6 %conditional.2 = (f32[2,6,192,128]{3,2,1,0:T(8,128)S(1)}, f32[2,6,192]{2,1,0:T(8,128)S(1)}, f32[2,6,192]{2,1,0:T(8,128)S(1)}, f32[2,6,192,128]{3,2,1,0:T(8,128)S...) conditional(s32[]{:T(128)} %convert_element_type.52, (bf16[384,2,128]{2,0,1:T(8,128)(2,1)S(1)}, ...), branch_computations={%region_5.7_spmd, %region_8.12_spmd} | conditional | flops 461251584 | bytes 18466920 | solution.py:62
  211.8 6.3 %collective-permute-done = bf16[384,2,128]{2,0,1:T(8,128)(2,1)S(1)} collective-permute-done((bf16[384,2,128]{2,0,1:T(8,128)(2,1)}, bf16[384,2,128]{2,0,1:T(8,128)(2,1)S(1)}, u32[]{:S(2)}, u32[]{:S(2)}) %collective-permute-start) | collective-permute-done | bytes 196640 | tf_op jit(solution)/shard_map/while/body/eval_jaxpr/ppermute | solution.py:60
  218.1 2.1 collective-permute-done.1
  220.2 3.6 %conditional.2 = (f32[2,6,192,128]{3,2,1,0:T(8,128)S(1)}, f32[2,6,192]{2,1,0:T(8,128)S(1)}, f32[2,6,192]{2,1,0:T(8,128)S(1)}, f32[2,6,192,128]{3,2,1,0:T(8,128)S...) conditional(s32[]{:T(128)} %convert_element_type.52, (bf16[384,2,128]{2,0,1:T(8,128)(2,1)S(1)}, ...), branch_computations={%region_5.7_spmd, %region_8.12_spmd} | conditional | flops 461251584 | bytes 18466920 | solution.py:62
  (248 shorter events, 97.6 us)
Async XLA Ops:
  0.6 1.6 copy-start.3
  2.2 4.2 %copy-start = (bf16[192,12,128]{2,0,1:T(8,128)(2,1)}, bf16[192,12,128]{2,0,1:T(8,128)(2,1)S(1)}, u32[]{:S(2)}) copy-start(bf16[192,12,128]{2,0,1:T(8,128)(2,1)S(1)} %get-tuple-element.456) | copy-start | bytes 1769476
  3.0 1.3 copy-start.4
  10.9 6.4 %collective-permute-start = (bf16[384,2,128]{2,0,1:T(8,128)(2,1)}, bf16[384,2,128]{2,0,1:T(8,128)(2,1)S(1)}, u32[]{:S(2)}, u32[]{:S(2)}) collective-permute-start(bf16[384,2,128]{2,0,1:T(8,128)(2,1)} %get-tuple-element.581), channel_id=1, source_target_pairs={{0,1},{1,2},{2,3},{3,4},{4,5},{5,6},{6,7},{7,8},{8,9},{9,10},{10,1... | collective-permute-start | bytes 589832 | tf_op jit(solution)/shard_map/while/body/eval_jaxpr/ppermute | solution.py:60
  11.0 8.4 %collective-permute-start.1 = (bf16[384,2,128]{2,0,1:T(8,128)(2,1)}, bf16[384,2,128]{2,0,1:T(8,128)(2,1)S(1)}, u32[]{:S(2)}, u32[]{:S(2)}) collective-permute-start(bf16[384,2,128]{2,0,1:T(8,128)(2,1)} %get-tuple-element.582), channel_id=1, source_target_pairs={{0,1},{1,2},{2,3},{3,4},{4,5},{5,6},{6,7},{7,8},{8,9},{9,10},{10,1... | collective-permute-start | bytes 589832 | tf_op jit(solution)/shard_map/while/body/eval_jaxpr/ppermute | solution.py:60
  22.0 1.6 copy-start.1
  23.6 1.1 copy-start.2
  26.1 6.3 %collective-permute-start = (bf16[384,2,128]{2,0,1:T(8,128)(2,1)}, bf16[384,2,128]{2,0,1:T(8,128)(2,1)S(1)}, u32[]{:S(2)}, u32[]{:S(2)}) collective-permute-start(bf16[384,2,128]{2,0,1:T(8,128)(2,1)} %get-tuple-element.581), channel_id=1, source_target_pairs={{0,1},{1,2},{2,3},{3,4},{4,5},{5,6},{6,7},{7,8},{8,9},{9,10},{10,1... | collective-permute-start | bytes 589832 | tf_op jit(solution)/shard_map/while/body/eval_jaxpr/ppermute | solution.py:60
  26.1 8.4 %collective-permute-start.1 = (bf16[384,2,128]{2,0,1:T(8,128)(2,1)}, bf16[384,2,128]{2,0,1:T(8,128)(2,1)S(1)}, u32[]{:S(2)}, u32[]{:S(2)}) collective-permute-start(bf16[384,2,128]{2,0,1:T(8,128)(2,1)} %get-tuple-element.582), channel_id=1, source_target_pairs={{0,1},{1,2},{2,3},{3,4},{4,5},{5,6},{6,7},{7,8},{8,9},{9,10},{10,1... | collective-permute-start | bytes 589832 | tf_op jit(solution)/shard_map/while/body/eval_jaxpr/ppermute | solution.py:60
  37.1 1.6 copy-start.1
  38.7 1.1 copy-start.2
  41.2 6.3 %collective-permute-start = (bf16[384,2,128]{2,0,1:T(8,128)(2,1)}, bf16[384,2,128]{2,0,1:T(8,128)(2,1)S(1)}, u32[]{:S(2)}, u32[]{:S(2)}) collective-permute-start(bf16[384,2,128]{2,0,1:T(8,128)(2,1)} %get-tuple-element.581), channel_id=1, source_target_pairs={{0,1},{1,2},{2,3},{3,4},{4,5},{5,6},{6,7},{7,8},{8,9},{9,10},{10,1... | collective-permute-start | bytes 589832 | tf_op jit(solution)/shard_map/while/body/eval_jaxpr/ppermute | solution.py:60
  41.2 8.4 %collective-permute-start.1 = (bf16[384,2,128]{2,0,1:T(8,128)(2,1)}, bf16[384,2,128]{2,0,1:T(8,128)(2,1)S(1)}, u32[]{:S(2)}, u32[]{:S(2)}) collective-permute-start(bf16[384,2,128]{2,0,1:T(8,128)(2,1)} %get-tuple-element.582), channel_id=1, source_target_pairs={{0,1},{1,2},{2,3},{3,4},{4,5},{5,6},{6,7},{7,8},{8,9},{9,10},{10,1... | collective-permute-start | bytes 589832 | tf_op jit(solution)/shard_map/while/body/eval_jaxpr/ppermute | solution.py:60
  52.1 1.6 copy-start.1
  53.8 1.1 copy-start.2
  56.3 6.3 %collective-permute-start = (bf16[384,2,128]{2,0,1:T(8,128)(2,1)}, bf16[384,2,128]{2,0,1:T(8,128)(2,1)S(1)}, u32[]{:S(2)}, u32[]{:S(2)}) collective-permute-start(bf16[384,2,128]{2,0,1:T(8,128)(2,1)} %get-tuple-element.581), channel_id=1, source_target_pairs={{0,1},{1,2},{2,3},{3,4},{4,5},{5,6},{6,7},{7,8},{8,9},{9,10},{10,1... | collective-permute-start | bytes 589832 | tf_op jit(solution)/shard_map/while/body/eval_jaxpr/ppermute | solution.py:60
  56.3 8.4 %collective-permute-start.1 = (bf16[384,2,128]{2,0,1:T(8,128)(2,1)}, bf16[384,2,128]{2,0,1:T(8,128)(2,1)S(1)}, u32[]{:S(2)}, u32[]{:S(2)}) collective-permute-start(bf16[384,2,128]{2,0,1:T(8,128)(2,1)} %get-tuple-element.582), channel_id=1, source_target_pairs={{0,1},{1,2},{2,3},{3,4},{4,5},{5,6},{6,7},{7,8},{8,9},{9,10},{10,1... | collective-permute-start | bytes 589832 | tf_op jit(solution)/shard_map/while/body/eval_jaxpr/ppermute | solution.py:60
  67.2 1.6 copy-start.1
  68.9 1.1 copy-start.2
  71.4 6.3 %collective-permute-start = (bf16[384,2,128]{2,0,1:T(8,128)(2,1)}, bf16[384,2,128]{2,0,1:T(8,128)(2,1)S(1)}, u32[]{:S(2)}, u32[]{:S(2)}) collective-permute-start(bf16[384,2,128]{2,0,1:T(8,128)(2,1)} %get-tuple-element.581), channel_id=1, source_target_pairs={{0,1},{1,2},{2,3},{3,4},{4,5},{5,6},{6,7},{7,8},{8,9},{9,10},{10,1... | collective-permute-start | bytes 589832 | tf_op jit(solution)/shard_map/while/body/eval_jaxpr/ppermute | solution.py:60
  71.4 8.4 %collective-permute-start.1 = (bf16[384,2,128]{2,0,1:T(8,128)(2,1)}, bf16[384,2,128]{2,0,1:T(8,128)(2,1)S(1)}, u32[]{:S(2)}, u32[]{:S(2)}) collective-permute-start(bf16[384,2,128]{2,0,1:T(8,128)(2,1)} %get-tuple-element.582), channel_id=1, source_target_pairs={{0,1},{1,2},{2,3},{3,4},{4,5},{5,6},{6,7},{7,8},{8,9},{9,10},{10,1... | collective-permute-start | bytes 589832 | tf_op jit(solution)/shard_map/while/body/eval_jaxpr/ppermute | solution.py:60
  82.3 1.6 copy-start.1
  83.9 1.1 copy-start.2
  86.4 6.3 %collective-permute-start = (bf16[384,2,128]{2,0,1:T(8,128)(2,1)}, bf16[384,2,128]{2,0,1:T(8,128)(2,1)S(1)}, u32[]{:S(2)}, u32[]{:S(2)}) collective-permute-start(bf16[384,2,128]{2,0,1:T(8,128)(2,1)} %get-tuple-element.581), channel_id=1, source_target_pairs={{0,1},{1,2},{2,3},{3,4},{4,5},{5,6},{6,7},{7,8},{8,9},{9,10},{10,1... | collective-permute-start | bytes 589832 | tf_op jit(solution)/shard_map/while/body/eval_jaxpr/ppermute | solution.py:60
  86.5 8.4 %collective-permute-start.1 = (bf16[384,2,128]{2,0,1:T(8,128)(2,1)}, bf16[384,2,128]{2,0,1:T(8,128)(2,1)S(1)}, u32[]{:S(2)}, u32[]{:S(2)}) collective-permute-start(bf16[384,2,128]{2,0,1:T(8,128)(2,1)} %get-tuple-element.582), channel_id=1, source_target_pairs={{0,1},{1,2},{2,3},{3,4},{4,5},{5,6},{6,7},{7,8},{8,9},{9,10},{10,1... | collective-permute-start | bytes 589832 | tf_op jit(solution)/shard_map/while/body/eval_jaxpr/ppermute | solution.py:60
  97.4 1.6 copy-start.1
  99.0 1.1 copy-start.2
  101.5 6.3 %collective-permute-start = (bf16[384,2,128]{2,0,1:T(8,128)(2,1)}, bf16[384,2,128]{2,0,1:T(8,128)(2,1)S(1)}, u32[]{:S(2)}, u32[]{:S(2)}) collective-permute-start(bf16[384,2,128]{2,0,1:T(8,128)(2,1)} %get-tuple-element.581), channel_id=1, source_target_pairs={{0,1},{1,2},{2,3},{3,4},{4,5},{5,6},{6,7},{7,8},{8,9},{9,10},{10,1... | collective-permute-start | bytes 589832 | tf_op jit(solution)/shard_map/while/body/eval_jaxpr/ppermute | solution.py:60
  101.5 8.4 %collective-permute-start.1 = (bf16[384,2,128]{2,0,1:T(8,128)(2,1)}, bf16[384,2,128]{2,0,1:T(8,128)(2,1)S(1)}, u32[]{:S(2)}, u32[]{:S(2)}) collective-permute-start(bf16[384,2,128]{2,0,1:T(8,128)(2,1)} %get-tuple-element.582), channel_id=1, source_target_pairs={{0,1},{1,2},{2,3},{3,4},{4,5},{5,6},{6,7},{7,8},{8,9},{9,10},{10,1... | collective-permute-start | bytes 589832 | tf_op jit(solution)/shard_map/while/body/eval_jaxpr/ppermute | solution.py:60
  112.5 1.6 copy-start.1
  114.1 1.1 copy-start.2
  116.6 6.3 %collective-permute-start = (bf16[384,2,128]{2,0,1:T(8,128)(2,1)}, bf16[384,2,128]{2,0,1:T(8,128)(2,1)S(1)}, u32[]{:S(2)}, u32[]{:S(2)}) collective-permute-start(bf16[384,2,128]{2,0,1:T(8,128)(2,1)} %get-tuple-element.581), channel_id=1, source_target_pairs={{0,1},{1,2},{2,3},{3,4},{4,5},{5,6},{6,7},{7,8},{8,9},{9,10},{10,1... | collective-permute-start | bytes 589832 | tf_op jit(solution)/shard_map/while/body/eval_jaxpr/ppermute | solution.py:60
  116.6 8.4 %collective-permute-start.1 = (bf16[384,2,128]{2,0,1:T(8,128)(2,1)}, bf16[384,2,128]{2,0,1:T(8,128)(2,1)S(1)}, u32[]{:S(2)}, u32[]{:S(2)}) collective-permute-start(bf16[384,2,128]{2,0,1:T(8,128)(2,1)} %get-tuple-element.582), channel_id=1, source_target_pairs={{0,1},{1,2},{2,3},{3,4},{4,5},{5,6},{6,7},{7,8},{8,9},{9,10},{10,1... | collective-permute-start | bytes 589832 | tf_op jit(solution)/shard_map/while/body/eval_jaxpr/ppermute | solution.py:60
  127.6 1.6 copy-start.1
  131.7 6.3 %collective-permute-start = (bf16[384,2,128]{2,0,1:T(8,128)(2,1)}, bf16[384,2,128]{2,0,1:T(8,128)(2,1)S(1)}, u32[]{:S(2)}, u32[]{:S(2)}) collective-permute-start(bf16[384,2,128]{2,0,1:T(8,128)(2,1)} %get-tuple-element.581), channel_id=1, source_target_pairs={{0,1},{1,2},{2,3},{3,4},{4,5},{5,6},{6,7},{7,8},{8,9},{9,10},{10,1... | collective-permute-start | bytes 589832 | tf_op jit(solution)/shard_map/while/body/eval_jaxpr/ppermute | solution.py:60
  131.7 8.4 %collective-permute-start.1 = (bf16[384,2,128]{2,0,1:T(8,128)(2,1)}, bf16[384,2,128]{2,0,1:T(8,128)(2,1)S(1)}, u32[]{:S(2)}, u32[]{:S(2)}) collective-permute-start(bf16[384,2,128]{2,0,1:T(8,128)(2,1)} %get-tuple-element.582), channel_id=1, source_target_pairs={{0,1},{1,2},{2,3},{3,4},{4,5},{5,6},{6,7},{7,8},{8,9},{9,10},{10,1... | collective-permute-start | bytes 589832 | tf_op jit(solution)/shard_map/while/body/eval_jaxpr/ppermute | solution.py:60
  145.1 6.3 %collective-permute-start = (bf16[384,2,128]{2,0,1:T(8,128)(2,1)}, bf16[384,2,128]{2,0,1:T(8,128)(2,1)S(1)}, u32[]{:S(2)}, u32[]{:S(2)}) collective-permute-start(bf16[384,2,128]{2,0,1:T(8,128)(2,1)} %get-tuple-element.581), channel_id=1, source_target_pairs={{0,1},{1,2},{2,3},{3,4},{4,5},{5,6},{6,7},{7,8},{8,9},{9,10},{10,1... | collective-permute-start | bytes 589832 | tf_op jit(solution)/shard_map/while/body/eval_jaxpr/ppermute | solution.py:60
  145.1 8.4 %collective-permute-start.1 = (bf16[384,2,128]{2,0,1:T(8,128)(2,1)}, bf16[384,2,128]{2,0,1:T(8,128)(2,1)S(1)}, u32[]{:S(2)}, u32[]{:S(2)}) collective-permute-start(bf16[384,2,128]{2,0,1:T(8,128)(2,1)} %get-tuple-element.582), channel_id=1, source_target_pairs={{0,1},{1,2},{2,3},{3,4},{4,5},{5,6},{6,7},{7,8},{8,9},{9,10},{10,1... | collective-permute-start | bytes 589832 | tf_op jit(solution)/shard_map/while/body/eval_jaxpr/ppermute | solution.py:60
  158.4 6.3 %collective-permute-start = (bf16[384,2,128]{2,0,1:T(8,128)(2,1)}, bf16[384,2,128]{2,0,1:T(8,128)(2,1)S(1)}, u32[]{:S(2)}, u32[]{:S(2)}) collective-permute-start(bf16[384,2,128]{2,0,1:T(8,128)(2,1)} %get-tuple-element.581), channel_id=1, source_target_pairs={{0,1},{1,2},{2,3},{3,4},{4,5},{5,6},{6,7},{7,8},{8,9},{9,10},{10,1... | collective-permute-start | bytes 589832 | tf_op jit(solution)/shard_map/while/body/eval_jaxpr/ppermute | solution.py:60
  158.4 8.4 %collective-permute-start.1 = (bf16[384,2,128]{2,0,1:T(8,128)(2,1)}, bf16[384,2,128]{2,0,1:T(8,128)(2,1)S(1)}, u32[]{:S(2)}, u32[]{:S(2)}) collective-permute-start(bf16[384,2,128]{2,0,1:T(8,128)(2,1)} %get-tuple-element.582), channel_id=1, source_target_pairs={{0,1},{1,2},{2,3},{3,4},{4,5},{5,6},{6,7},{7,8},{8,9},{9,10},{10,1... | collective-permute-start | bytes 589832 | tf_op jit(solution)/shard_map/while/body/eval_jaxpr/ppermute | solution.py:60
  171.8 6.3 %collective-permute-start = (bf16[384,2,128]{2,0,1:T(8,128)(2,1)}, bf16[384,2,128]{2,0,1:T(8,128)(2,1)S(1)}, u32[]{:S(2)}, u32[]{:S(2)}) collective-permute-start(bf16[384,2,128]{2,0,1:T(8,128)(2,1)} %get-tuple-element.581), channel_id=1, source_target_pairs={{0,1},{1,2},{2,3},{3,4},{4,5},{5,6},{6,7},{7,8},{8,9},{9,10},{10,1... | collective-permute-start | bytes 589832 | tf_op jit(solution)/shard_map/while/body/eval_jaxpr/ppermute | solution.py:60
  171.8 8.4 %collective-permute-start.1 = (bf16[384,2,128]{2,0,1:T(8,128)(2,1)}, bf16[384,2,128]{2,0,1:T(8,128)(2,1)S(1)}, u32[]{:S(2)}, u32[]{:S(2)}) collective-permute-start(bf16[384,2,128]{2,0,1:T(8,128)(2,1)} %get-tuple-element.582), channel_id=1, source_target_pairs={{0,1},{1,2},{2,3},{3,4},{4,5},{5,6},{6,7},{7,8},{8,9},{9,10},{10,1... | collective-permute-start | bytes 589832 | tf_op jit(solution)/shard_map/while/body/eval_jaxpr/ppermute | solution.py:60
  185.1 6.3 %collective-permute-start = (bf16[384,2,128]{2,0,1:T(8,128)(2,1)}, bf16[384,2,128]{2,0,1:T(8,128)(2,1)S(1)}, u32[]{:S(2)}, u32[]{:S(2)}) collective-permute-start(bf16[384,2,128]{2,0,1:T(8,128)(2,1)} %get-tuple-element.581), channel_id=1, source_target_pairs={{0,1},{1,2},{2,3},{3,4},{4,5},{5,6},{6,7},{7,8},{8,9},{9,10},{10,1... | collective-permute-start | bytes 589832 | tf_op jit(solution)/shard_map/while/body/eval_jaxpr/ppermute | solution.py:60
  185.1 8.4 %collective-permute-start.1 = (bf16[384,2,128]{2,0,1:T(8,128)(2,1)}, bf16[384,2,128]{2,0,1:T(8,128)(2,1)S(1)}, u32[]{:S(2)}, u32[]{:S(2)}) collective-permute-start(bf16[384,2,128]{2,0,1:T(8,128)(2,1)} %get-tuple-element.582), channel_id=1, source_target_pairs={{0,1},{1,2},{2,3},{3,4},{4,5},{5,6},{6,7},{7,8},{8,9},{9,10},{10,1... | collective-permute-start | bytes 589832 | tf_op jit(solution)/shard_map/while/body/eval_jaxpr/ppermute | solution.py:60
  198.5 6.3 %collective-permute-start = (bf16[384,2,128]{2,0,1:T(8,128)(2,1)}, bf16[384,2,128]{2,0,1:T(8,128)(2,1)S(1)}, u32[]{:S(2)}, u32[]{:S(2)}) collective-permute-start(bf16[384,2,128]{2,0,1:T(8,128)(2,1)} %get-tuple-element.581), channel_id=1, source_target_pairs={{0,1},{1,2},{2,3},{3,4},{4,5},{5,6},{6,7},{7,8},{8,9},{9,10},{10,1... | collective-permute-start | bytes 589832 | tf_op jit(solution)/shard_map/while/body/eval_jaxpr/ppermute | solution.py:60
  198.5 8.4 %collective-permute-start.1 = (bf16[384,2,128]{2,0,1:T(8,128)(2,1)}, bf16[384,2,128]{2,0,1:T(8,128)(2,1)S(1)}, u32[]{:S(2)}, u32[]{:S(2)}) collective-permute-start(bf16[384,2,128]{2,0,1:T(8,128)(2,1)} %get-tuple-element.582), channel_id=1, source_target_pairs={{0,1},{1,2},{2,3},{3,4},{4,5},{5,6},{6,7},{7,8},{8,9},{9,10},{10,1... | collective-permute-start | bytes 589832 | tf_op jit(solution)/shard_map/while/body/eval_jaxpr/ppermute | solution.py:60
  211.8 6.3 %collective-permute-start = (bf16[384,2,128]{2,0,1:T(8,128)(2,1)}, bf16[384,2,128]{2,0,1:T(8,128)(2,1)S(1)}, u32[]{:S(2)}, u32[]{:S(2)}) collective-permute-start(bf16[384,2,128]{2,0,1:T(8,128)(2,1)} %get-tuple-element.581), channel_id=1, source_target_pairs={{0,1},{1,2},{2,3},{3,4},{4,5},{5,6},{6,7},{7,8},{8,9},{9,10},{10,1... | collective-permute-start | bytes 589832 | tf_op jit(solution)/shard_map/while/body/eval_jaxpr/ppermute | solution.py:60
  211.8 8.4 %collective-permute-start.1 = (bf16[384,2,128]{2,0,1:T(8,128)(2,1)}, bf16[384,2,128]{2,0,1:T(8,128)(2,1)S(1)}, u32[]{:S(2)}, u32[]{:S(2)}) collective-permute-start(bf16[384,2,128]{2,0,1:T(8,128)(2,1)} %get-tuple-element.582), channel_id=1, source_target_pairs={{0,1},{1,2},{2,3},{3,4},{4,5},{5,6},{6,7},{7,8},{8,9},{9,10},{10,1... | collective-permute-start | bytes 589832 | tf_op jit(solution)/shard_map/while/body/eval_jaxpr/ppermute | solution.py:60
  (1 other events, 1.1 us)
where the time goes:
time: 229 us; the launch traced here: 228 us
  waiting for transfers between devices  125 us (55%)
  matrix products  55.5 us (24%)
  local copies, waits for them, and re-layouts  23.8 us (10%)
  other arithmetic  20.2 us (9%)
    ppermute x30, waiting for transfers between devices, hop(): k_cur, v_cur = lax.ppermute((k_cur, v_cur), 'cp', shift_pairs)  125 us
    dot_general x25, matrix products, attend_update(): jnp.einsum('hgqk,khd->hgqd', expd.astype(jnp.bfloat16), v_blk, preferred_...  31.4 us
    dot_general x25, matrix products, attend_update(): jnp.einsum('qhgd,khd->hgqk', q_blk, k_blk, preferred_element_type=jnp.flo...  24.1 us
    while x45, local copies, waits for them, and re-layouts  20.3 us
    reduce_sum x25, other arithmetic, attend_update(): new_sum = row_sum * rescale + jnp.sum(expd, axis=-1)  17.5 us
  transfers between devices with their start and end apart: 30, of which 30 were waited for; matrix products, arithmetic and copies ran while one was open for 0% of the time, Pallas kernels for 0%

commit v1 on v0

v1 whole, which is shorter than its diff:
```python
import functools
import math

import jax
import jax.numpy as jnp
from jax import lax
from jax.experimental import pallas as pl
from jax.experimental.pallas import tpu as pltpu
from jax.sharding import PartitionSpec as P

MESH = pl.DeviceIdType.MESH
F32 = jnp.float32
UP, DOWN = 0, 1
LANES = 256


def attention_kernel(n_cp, q_ref, own_ref, o_ref, lse_ref, kv_buf, acc_ref, max_ref, sum_ref,
                     send_sem, recv_sem, pair_send, pair_recv, own_sem):
    n_z = n_cp // 2
    n_round = n_z - 1
    _, kv_heads, _, half_len, head_dim = own_ref.shape
    group = q_ref.shape[0] // kv_heads
    rows = group * half_len
    coef = head_dim ** -0.5 * math.log2(math.e)
    me = lax.axis_index("cp")
    z, core = me // 2, me % 2
    above = lax.rem(z + 1, n_z) * 2 + core
    below = lax.rem(z + n_z - 1, n_z) * 2 + core
    partner = z * 2 + 1 - core

    barrier = pltpu.get_barrier_semaphore()
    for other in (above, below, partner):
        pl.semaphore_signal(barrier, inc=1, device_id={"cp": other}, device_id_type=MESH)
    pl.semaphore_wait(barrier, 3)

    def ring_copy(src, chip, part, way, index):
        return pltpu.make_async_remote_copy(
            src_ref=src, dst_ref=kv_buf.at[part, chip, core],
            send_sem=send_sem.at[way, index], recv_sem=recv_sem.at[way, index],
            device_id={"cp": above if way == UP else below}, device_id_type=MESH)

    def pair_copy(src, chip, part, way, index):
        return pltpu.make_async_remote_copy(
            src_ref=src, dst_ref=kv_buf.at[part, chip, core],
            send_sem=pair_send.at[way, index], recv_sem=pair_recv.at[way, index],
            device_id={"cp": partner}, device_id_type=MESH)

    def pair_wait(chip, part, way, index):
        pltpu.make_async_remote_copy(
            src_ref=kv_buf.at[part, chip, 1 - core], dst_ref=kv_buf.at[part, chip, 1 - core],
            send_sem=pair_send.at[way, index], recv_sem=pair_recv.at[way, index],
            device_id={"cp": partner}, device_id_type=MESH).wait_recv()

    own_copies = [pltpu.make_async_copy(own_ref.at[part], kv_buf.at[part, z, core], own_sem.at[part])
                  for part in range(2)]
    for part in range(2):
        for way in (UP, DOWN):
            ring_copy(own_ref.at[part], z, part, way, part).start()
        pair_copy(own_ref.at[part], z, part, part, n_round).start()
        own_copies[part].start()

    acc_ref[...] = jnp.zeros_like(acc_ref)
    max_ref[...] = jnp.full_like(max_ref, -jnp.inf)
    sum_ref[...] = jnp.zeros_like(sum_ref)

    tiles = [(head, start, min(LANES, rows - start))
             for head in range(kv_heads) for start in range(0, rows, LANES)]

    def job(chip, part, half, key_pos=None, query_base=None):
        def keys(head, which):
            return kv_buf[part, chip, :, head, which].reshape(2 * half_len, head_dim)

        def scores(tile):
            head, start, size = tile
            q_all = q_ref[head * group:(head + 1) * group, half].reshape(rows, head_dim)
            s = lax.dot_general(keys(head, 0), q_all[start:start + size], (((1,), (1,)), ((), ())),
                                preferred_element_type=F32)
            if key_pos is not None:
                lane = lax.broadcasted_iota(jnp.int32, (1, size), 1) + start
                q_pos = query_base + lane % half_len
                s = jnp.where(key_pos <= q_pos, s, -jnp.inf)
            return s

        ahead = scores(tiles[0])
        for n, (head, start, size) in enumerate(tiles):
            s = ahead
            if n + 1 < len(tiles):
                ahead = scores(tiles[n + 1])
            cols = slice(start, start + size)
            v_t = keys(head, 1).T
            old = max_ref[half, head, :, cols]
            new = jnp.maximum(old, jnp.max(s, axis=0, keepdims=True))
            p = jnp.exp2((s - new) * coef)
            alpha = jnp.exp2((old - new) * coef)
            max_ref[half, head, :, cols] = new
            part_sum = jnp.sum(p.reshape(-1, 8, size), axis=0)
            sum_ref[half, head, :, cols] = sum_ref[half, head, :, cols] * alpha + part_sum
            acc_ref[half, head, :, cols] = acc_ref[half, head, :, cols] * alpha + jnp.dot(
                v_t, p.astype(jnp.bfloat16), preferred_element_type=F32)

    for part in range(2):
        own_copies[part].wait()
        pair_wait(z, part, part, n_round)

    job(z, 0, 1)
    row_id = lax.broadcasted_iota(jnp.int32, (2 * half_len, 1), 0)

    def own_job(part, carry):
        first_block = jnp.where(part == 0, 2 * z, 2 * n_cp - 1 - 2 * z)
        shift = jnp.where(part == 0, 0, 2 * half_len)
        key_pos = first_block * half_len + row_id - jnp.where(row_id >= half_len, shift, 0)
        query_block = jnp.where(part == 0, me, 2 * n_cp - 1 - me)
        job(z, part, part, key_pos, query_block * half_len)
        return carry

    lax.fori_loop(0, 2, own_job, 0)

    def source(rnd, way):
        step = rnd // 2 + 1
        chip = lax.rem(z + n_z - step, n_z) if way == UP else lax.rem(z + step, n_z)
        part = jnp.where(rnd == n_round - 1, way, rnd % 2)
        return chip, part

    def remote_round(rnd, carry):
        for way in (UP, DOWN):
            chip, part = source(rnd, way)
            block = kv_buf.at[part, chip, core]
            ring_copy(block, chip, part, way, rnd).wait_recv()
            pair_copy(block, chip, part, way, rnd).start()
            last_forward = n_round - 3 if way == UP else n_round - 2

            @pl.when((rnd < n_round - 3) | (rnd == last_forward))
            def _():
                ring_copy(block, chip, part, way, jnp.minimum(rnd + 2, n_round - 1)).start()
        for way in (UP, DOWN):
            chip, part = source(rnd, way)
            pair_wait(chip, part, way, rnd)

        def one_job(way, inner):
            step = rnd // 2 + 1
            chip = lax.rem(z + n_z + jnp.where(way == UP, -step, step), n_z)
            kind = jnp.where(rnd == n_round - 1, way, rnd % 2)
            lower = jnp.where(chip < z, 1, 0)
            job(chip, kind * (1 - lower), 1 - kind * lower)
            return inner

        lax.fori_loop(0, 2, one_job, 0)
        return carry

    lax.fori_loop(0, n_round, remote_round, 0)

    for half in range(2):
        for head in range(kv_heads):
            total = jnp.sum(sum_ref[half, head], axis=0, keepdims=True)
            lse = max_ref[half, head] * head_dim ** -0.5 + jnp.log(total)
            inverse = 1.0 / total
            for g in range(group):
                lse_ref[head * group + g, half] = lse[0, g * half_len:(g + 1) * half_len]
            out = (acc_ref[half, head] * inverse).T.astype(jnp.bfloat16)
            o_ref[head * group:(head + 1) * group, half] = out.reshape(group, half_len, head_dim)

    for rnd in range(n_round):
        for way in (UP, DOWN):
            chip, part = source(rnd, way)
            block = kv_buf.at[part, chip, core]
            ring_copy(block, chip, part, way, rnd).wait_send()
            pair_copy(block, chip, part, way, rnd).wait_send()
    for part in range(2):
        pair_copy(own_ref.at[part], z, part, part, n_round).wait_send()


def solution(mesh):
    n_cp = mesh.shape["cp"]
    row_spec = P(("dp", "cp"), None, None)
    lse_spec = P(("dp", "cp"), None)

    def local_attention(q_tok, k_tok, v_tok):
        tok_count, q_heads, head_dim = q_tok.shape
        kv_heads = k_tok.shape[1]
        group = q_heads // kv_heads
        half_len = tok_count // 2
        rows = group * half_len
        q_in = q_tok.transpose(1, 0, 2).reshape(q_heads, 2, half_len, head_dim)
        kv = jnp.stack([k_tok, v_tok]).reshape(2, 2, half_len, kv_heads, head_dim)
        own = kv.transpose(1, 3, 0, 2, 4)
        vmem = pl.BlockSpec(memory_space=pltpu.VMEM)
        out, lse = pl.pallas_call(
            functools.partial(attention_kernel, n_cp),
            out_shape=(jax.ShapeDtypeStruct((q_heads, 2, half_len, head_dim), jnp.bfloat16),
                       jax.ShapeDtypeStruct((q_heads, 2, half_len), F32)),
            in_specs=[vmem, vmem],
            out_specs=(vmem, vmem),
            scratch_shapes=[
                pltpu.VMEM((2, n_cp // 2, 2, kv_heads, 2, half_len, head_dim), jnp.bfloat16),
                pltpu.VMEM((2, kv_heads, head_dim, rows), F32),
                pltpu.VMEM((2, kv_heads, 1, rows), F32),
                pltpu.VMEM((2, kv_heads, 8, rows), F32),
                pltpu.SemaphoreType.DMA((2, n_cp // 2 - 1)),
                pltpu.SemaphoreType.DMA((2, n_cp // 2 - 1)),
                pltpu.SemaphoreType.DMA((2, n_cp // 2)),
                pltpu.SemaphoreType.DMA((2, n_cp // 2)),
                pltpu.SemaphoreType.DMA((2,)),
            ],
            compiler_params=pltpu.CompilerParams(collective_id=0, has_side_effects=True,
                                                 vmem_limit_bytes=48 * 1024 * 1024),
        )(q_in, own)
        out_tok = out.reshape(q_heads, tok_count, head_dim).transpose(1, 0, 2)
        return out_tok, lse.reshape(q_heads, tok_count).T

    return jax.shard_map(local_attention, mesh=mesh, in_specs=(row_spec, row_spec, row_spec),
                         out_specs=(row_spec, lse_spec), check_vma=False)
```

time: 229 us -> 57.7 us (0.25)
  the two profiles are of different devices: /device:TPU:148 before, /device:TPU:21 now
where the time goes in v1:
time: 57.7 us; the launch traced here: 57.6 us
  Pallas kernels  53.2 us (92%)
  local copies, waits for them, and re-layouts  3.72 us (6%)
  between operations  0.67 us (1%)
    pallas_call x1, Pallas kernels, local_attention(): pl.pallas_call(functools.partial(attention_kernel, n_cp), out_shape=(jax....  53.2 us
    another operation x2, local copies, waits for them, and re-layouts, local_attention(): kv = jnp.stack([k_tok, v_tok]).reshape(2, 2, half_len, kv_heads, head_dim)  2.01 us

profile of v1, /device:TPU:21, one launch (start us, length us, event | category | flops | bytes accessed | tf_op | source)
XLA Modules:
  0.0 57.6 jit_solution(8130389017358451312)
XLA Ops:
  0.6 0.0 copy-start
  0.6 1.0 %copy.7 = bf16[1,2,192,2,128]{4,2,0,3,1:T(8,128)(2,1)S(1)} copy(bf16[1,2,192,2,128]{4,3,2,1,0:T(2,128)(2,1)} %bitcast.13) | data formatting | bytes 393216 | tf_op jit(solution)/shard_map/stack | solution.py:184
  1.7 1.0 %copy.8 = bf16[1,2,192,2,128]{4,2,0,3,1:T(8,128)(2,1)S(1)} copy(bf16[1,2,192,2,128]{4,3,2,1,0:T(2,128)(2,1)} %bitcast.14) | data formatting | bytes 393216 | tf_op jit(solution)/shard_map/stack | solution.py:184
  2.7 0.0 copy-done
  2.7 53.2 %shard_map.50 = (bf16[12,2,192,128]{3,2,1,0:T(8,128)(2,1)S(1)}, f32[12,2,192]{2,1,0:T(2,128)S(1)}) custom-call(bf16[12,2,192,128]{3,2,1,0:T(8,128)(2,1)S(1)} %bitcast.11, bf16[2,2,2,192,128]{4,3,2,1,0:T(8,128)(2,1)S(1)} %maximum_bitcast_fusion.own_ref), custom_call_target="tpu_custom_call" | custom-call | tf_op jit(solution)/shard_map/pallas_call | solution.py:187
  55.9 0.7 %reshape.20 = f32[12,384]{1,0:T(8,128)} reshape(f32[12,2,192]{2,1,0:T(2,128)S(1)} %get-tuple-element.5) | data formatting | bytes 36864 | tf_op jit(solution)/shard_map/reshape | solution.py:208
  56.6 1.0 %copy.14 = bf16[384,12,128]{2,0,1:T(8,128)(2,1)} copy(bf16[384,12,128]{2,0,1:T(8,128)(2,1)S(1)} %bitcast.12) | data formatting | bytes 2359296
  (1 shorter events, 0.0 us)
Async XLA Ops:
  0.6 2.1 %copy-start = (bf16[384,12,128]{2,0,1:T(8,128)(2,1)S(1)}, bf16[384,12,128]{2,0,1:T(8,128)(2,1)}, u32[]{:S(2)}) copy-start(bf16[384,12,128]{2,0,1:T(8,128)(2,1)} %param.3) | copy-start | bytes 3538948
